TPU v7x, 16 devices: a 4x2x1 block of a 4x4x8 slice. The times are simulated.
16 devices in a mesh: dp: 2 (over y, z), tp: 8 (over x, core).
Axes of the slice: x: 4, y: 2, z: 1, core: 2. Of those that a mesh axis runs over, the one named last changes fastest.
The devices are a block of a 4x4x8 slice.
Arguments:
- x: bfloat16 [5632, 3072], P(('dp', 'tp')), parts along dimension 0
- w_gate: bfloat16 [3072, 8192], P(None, 'tp')
- w_up: bfloat16 [3072, 8192], P(None, 'tp')
- w_down: bfloat16 [8192, 3072], P('tp')
Outputs:
- output: bfloat16 [5632, 3072], P(('dp', 'tp')), parts along dimension 0
There are 2 independent parts. A program takes and returns all parts, laid end to end along the dimension named above; an argument that names none is the same for every part.
All inputs are finite; a program needn't handle non-finite values.
Results may differ from a plain program's by a relative error of at most 0.016.
Values are sent between devices in bfloat16 or wider.
A program may use at most 768 MiB of HBM per device.

v0:
```python
import jax
import jax.numpy as jnp
from jax import lax
from jax.sharding import PartitionSpec as P


def solution(mesh):
    def step(x, w_gate, w_up, w_down):
        rows = lax.all_gather(x, "tp", axis=0, tiled=True)
        gate = jnp.dot(rows, w_gate, preferred_element_type=jnp.float32)
        up = jnp.dot(rows, w_up, preferred_element_type=jnp.float32)
        hidden = (jax.nn.silu(gate) * up).astype(jnp.bfloat16)
        term = jnp.dot(hidden, w_down, preferred_element_type=jnp.float32).astype(jnp.bfloat16)
        return lax.psum_scatter(term, "tp", scatter_dimension=0, tiled=True)

    return jax.shard_map(
        step,
        mesh=mesh,
        in_specs=(P(("dp", "tp"), None), P(None, "tp"), P(None, "tp"), P("tp", None)),
        out_specs=P(("dp", "tp"), None),
        check_vma=False,
    )
```

profile of v0, /device:TPU:112, one launch (start us, length us, event | category | flops | bytes accessed | tf_op | source)
XLA Modules:
  0.0 267.9 jit_solution(12310324285693104014)
XLA Ops:
  6.5 0.0 all-gather.2.cloned.1.call-start
  6.6 0.7 all-gather.2.cloned.1.call-update
  7.3 0.1 reduce-scatter.2.cloned.1.call-start
  7.4 87.7 %all-gather.2.cloned.1.call-done = bf16[2816,3072]{1,0:T(8,128)(2,1)} async-done(((bf16[352,3072]{1,0:T(8,128)(2,1)}), bf16[2816,3072]{1,0:T(8,128)(2,1)}) %all-gather.2.cloned.1.call-update) | async-done | bytes 17301520 | tf_op jit(solution)/shard_map/all_gather | solution.py:9
  95.1 0.0 copy-start
  95.1 24.3 %fusion.1 = f32[2816,1024]{1,0:T(8,128)} fusion(bf16[2816,3072]{1,0:T(8,128)(2,1)} %all-gather.2.cloned.1.call-done, bf16[3072,1024]{1,0:T(8,128)(2,1)} %param.5), kind=kOutput, calls=%fused_computation.3 | convolution fusion | flops 17716740096 | bytes 35127296 | tf_op jit(solution)/shard_map/dot_general | solution.py:10
  119.4 0.0 copy-done
  119.4 26.2 %multiply_convert_fusion.clone.4 = bf16[2816,1024]{1,0:T(8,128)(2,1)} fusion(f32[2816,1024]{1,0:T(8,128)} %fusion.1, bf16[2816,3072]{1,0:T(8,128)(2,1)S(1)} %copy-done, bf16[3072,1024]{1,0:T(8,128)(2,1)} %param.6), kind=kOutput, calls=%fused_computation.1.clone.clone.clone.1 | convolution fusion | flops 17734041600 | bytes 40894464 | tf_op jit(solution)/shard_map/dot_general | solution.py:11
  145.6 24.5 %convolution_convert_fusion = bf16[2816,3072]{1,0:T(8,128)(2,1)} fusion(bf16[1024,3072]{1,0:T(8,128)(2,1)} %param.7, bf16[2816,1024]{1,0:T(8,128)(2,1)} %multiply_convert_fusion.clone.4), kind=kOutput, calls=%fused_computation | convolution fusion | flops 17725390848 | bytes 29360128 | tf_op jit(solution)/shard_map/dot_general | solution.py:13
  170.1 0.1 reduce-scatter.2.cloned.1.call-update
  170.1 90.9 %reduce-scatter.2.cloned.1.call-done = bf16[352,3072]{1,0:T(8,128)(2,1)} async-done(((bf16[2816,3072]{1,0:T(8,128)(2,1)}), bf16[352,3072]{1,0:T(8,128)(2,1)}) %reduce-scatter.2.cloned.1.call-update) | async-done | bytes 2162704 | tf_op jit(solution)/shard_map/reduce_scatter | solution.py:14
Async XLA Ops:
  6.5 88.6 %all-gather.2.cloned.1.call-start = ((), (), s32[]{:S(2)}) async-start(), calls=%async_computation.1 | async-start | bytes 19464192 | tf_op jit(solution)/shard_map/all_gather | solution.py:9
  7.3 253.7 %reduce-scatter.2.cloned.1.call-start = ((), (), s32[]{:S(2)}) async-start(), calls=%async_computation.2 | async-start | bytes 19464192 | tf_op jit(solution)/shard_map/reduce_scatter | solution.py:14
  95.1 24.3 %copy-start = (bf16[2816,3072]{1,0:T(8,128)(2,1)S(1)}, bf16[2816,3072]{1,0:T(8,128)(2,1)}, u32[]{:S(2)}) copy-start(bf16[2816,3072]{1,0:T(8,128)(2,1)} %all-gather.2.cloned.1.call-done) | copy-start | bytes 51904516
Sparse Core Ops, SparseCore 0:
  8.9 86.1 all-gather.1
  170.3 90.7 reduce-scatter.1
where the time goes:
time: 268 us
  waiting for transfers between devices  179 us (67%)
  matrix products  75 us (28%)
  between operations  13.4 us (5%)
    reduce_scatter x1, waiting for transfers between devices, step(): return lax.psum_scatter(term, 'tp', scatter_dimension=0, tiled=True)  90.9 us
    all_gather x1, waiting for transfers between devices, step(): rows = lax.all_gather(x, 'tp', axis=0, tiled=True)  87.7 us
    dot_general x1, matrix products, step(): up = jnp.dot(rows, w_up, preferred_element_type=jnp.float32)  26.2 us
    dot_general x1, matrix products, step(): jnp.dot(hidden, w_down, preferred_element_type=jnp.float32)  24.5 us
    dot_general x1, matrix products, step(): gate = jnp.dot(rows, w_gate, preferred_element_type=jnp.float32)  24.3 us
  transfers between devices with their start and end apart: 2, of which 2 were waited for; matrix products, arithmetic and copies ran while one was open for 0% of the time, Pallas kernels for 0%

commit v1 on v0

v1 whole, which is shorter than its diff:
```python
import functools

import jax
import jax.numpy as jnp
from jax import lax
from jax.experimental import pallas as pl
from jax.experimental.pallas import tpu as pltpu
from jax.sharding import PartitionSpec as P

F32, BF16 = jnp.float32, jnp.bfloat16

HIDDEN_TILE = 256
MODEL_TILE = 768


def tile(n, width):
    return pl.ds(pl.multiple_of(n * width, width), width)


def kernel(
    devices, x_hbm, wg_hbm, wu_hbm, wd_hbm, y_hbm,
    wg, wu, wd, xb, sib, first, pure, second, out, work, kept,
    load_sem, ag_send, ag_recv, pass_send, pass_recv,
    sib_send, sib_recv, first_send, first_recv, pure_send, pure_recv, second_send, second_recv, y_sem,
):
    rows = x_hbm.shape[0]
    half = rows // 2
    hidden, model = wd.shape
    hidden_tiles, model_tiles = hidden // HIDDEN_TILE, model // MODEL_TILE
    chips = devices // 2

    me = lax.axis_index("tp")
    chip, core = me // 2, lax.rem(me, 2)
    right = {"tp": lax.rem(chip + 1, chips) * 2 + core}
    left = {"tp": lax.rem(chip + chips - 1, chips) * 2 + core}
    sibling = {"tp": chip * 2 + 1 - core}

    theirs, ours = pl.ds(0, rows), pl.ds(rows, rows)
    lo, hi = pl.ds(rows, half), pl.ds(rows + half, half)

    def remote(src, dst, send, recv, to):
        return pltpu.make_async_remote_copy(
            src_ref=src, dst_ref=dst, send_sem=send, recv_sem=recv, device_id=to, device_id_type=pl.DeviceIdType.MESH
        )

    loads = [
        pltpu.make_async_copy(src, dst, load_sem.at[i])
        for i, (src, dst) in enumerate([(x_hbm, xb.at[0, ours]), (wg_hbm, wg), (wu_hbm, wu), (wd_hbm, wd)])
    ]
    for load in loads:
        load.start()

    barrier = pltpu.get_barrier_semaphore()
    for peer in (left, right, sibling):
        pl.semaphore_signal(barrier, inc=1, device_id=peer, device_id_type=pl.DeviceIdType.MESH)
    pl.semaphore_wait(barrier, 3)
    loads[0].wait()

    gather = [
        remote(xb.at[0, lo], xb.at[1, lo], ag_send.at[0], ag_recv.at[0], right),
        remote(xb.at[0, hi], xb.at[1, hi], ag_send.at[1], ag_recv.at[1], left),
        remote(xb.at[0, hi], xb.at[2, lo], ag_send.at[2], ag_recv.at[2], right),
        remote(xb.at[0, lo], xb.at[2, hi], ag_send.at[3], ag_recv.at[3], left),
        remote(xb.at[1, lo], xb.at[3, lo], ag_send.at[4], ag_recv.at[4], right),
        remote(xb.at[1, hi], xb.at[3, hi], ag_send.at[5], ag_recv.at[5], left),
    ]
    passes = [
        remote(xb.at[q, ours], xb.at[q, theirs], pass_send.at[q], pass_recv.at[q], sibling) for q in range(4)
    ]
    for copy in gather[:4]:
        copy.start()
    passes[0].start()

    def gate_up(q, keep):
        @pl.loop(0, hidden_tiles)
        def _(n):
            cols = tile(n, HIDDEN_TILE)
            gate = jnp.dot(xb[q], wg[:, cols], preferred_element_type=F32)
            up = jnp.dot(xb[q], wu[:, cols], preferred_element_type=F32)
            h = (jax.nn.silu(gate) * up).astype(BF16)
            work[:, cols] = h[:rows]
            kept[keep, :, cols] = h[rows:]

    def to_sibling(q, n):
        cols = tile(n, MODEL_TILE)
        return remote(xb.at[q, theirs, cols], sib.at[q, :, cols], sib_send.at[q, n], sib_recv.at[q, n], sibling)

    def down_theirs(q):
        @pl.loop(0, model_tiles)
        def _(n):
            cols = tile(n, MODEL_TILE)
            term = jnp.dot(work[...], wd[:, cols], preferred_element_type=F32)
            xb[q, theirs, cols] = term.astype(BF16)
            to_sibling(q, n).start()

    def pair_sum(q, keep, n):
        cols = tile(n, MODEL_TILE)
        term = jnp.dot(kept[keep], wd[:, cols], preferred_element_type=F32)
        to_sibling(q, n).wait_recv()
        return term + sib[q, :, cols].astype(F32)

    top, bottom = pl.ds(0, half), pl.ds(half, half)

    def hops(src, q, dst, send, recv, n, lo_to, hi_to, lo_rows, hi_rows):
        cols = tile(n, MODEL_TILE)
        if q is None:
            lo_src, hi_src = src.at[top, cols], src.at[bottom, cols]
        else:
            lo_src, hi_src = src.at[q, lo, cols], src.at[q, hi, cols]
        return (
            remote(lo_src, dst.at[lo_rows, cols], send.at[0, n], recv.at[0, n], lo_to),
            remote(hi_src, dst.at[hi_rows, cols], send.at[1, n], recv.at[1, n], hi_to),
        )

    def pure_hops(n):
        return hops(out, None, pure, pure_send, pure_recv, n, left, right, top, bottom)

    def first_hops(n):
        return hops(xb, 3, first, first_send, first_recv, n, right, left, bottom, top)

    def second_hops(n):
        return hops(xb, 2, second, second_send, second_recv, n, left, right, bottom, top)

    for load in loads[1:]:
        load.wait()
    passes[0].wait_recv()
    gate_up(0, 0)
    down_theirs(0)

    for copy in gather[:2]:
        copy.wait_recv()
    for copy in gather[4:]:
        copy.start()
    passes[1].start()
    passes[1].wait_recv()
    gate_up(1, 2)
    down_theirs(1)

    @pl.loop(0, model_tiles)
    def _(n):
        out[:, tile(n, MODEL_TILE)] = pair_sum(1, 2, n).astype(BF16)
        for copy in pure_hops(n):
            copy.start()

    for copy in gather[2:4]:
        copy.wait_recv()
    passes[2].start()
    passes[2].wait_recv()
    gate_up(2, 1)
    down_theirs(2)

    for copy in gather[4:]:
        copy.wait_recv()
    passes[3].start()
    passes[3].wait_recv()
    gate_up(3, 2)
    down_theirs(3)
    passes[3].wait_send()

    @pl.loop(0, model_tiles)
    def _(n):
        xb[3, ours, tile(n, MODEL_TILE)] = pair_sum(3, 2, n).astype(BF16)
        for copy in first_hops(n):
            copy.start()

    passes[2].wait_send()

    @pl.loop(0, model_tiles)
    def _(n):
        cols = tile(n, MODEL_TILE)
        total = pair_sum(2, 1, n)
        for copy in first_hops(n):
            copy.wait_recv()
        xb[2, ours, cols] = (total + first[:, cols].astype(F32)).astype(BF16)
        for copy in second_hops(n):
            copy.start()

    for copy in gather[:4]:
        copy.wait_send()
    passes[0].wait_send()

    def store(n):
        cols = tile(n, MODEL_TILE)
        return pltpu.make_async_copy(xb.at[0, ours, cols], y_hbm.at[:, cols], y_sem.at[n])

    @pl.loop(0, model_tiles)
    def _(n):
        cols = tile(n, MODEL_TILE)
        total = pair_sum(0, 0, n)
        for copy in pure_hops(n):
            copy.wait_recv()
        total = total + pure[:, cols].astype(F32)
        for copy in second_hops(n):
            copy.wait_recv()
        xb[0, ours, cols] = (total + second[:, cols].astype(F32)).astype(BF16)
        store(n).start()

    for copy in gather[4:]:
        copy.wait_send()
    passes[1].wait_send()

    @pl.loop(0, model_tiles)
    def _(n):
        for q in range(4):
            to_sibling(q, n).wait_send()
        for copy in (*pure_hops(n), *first_hops(n), *second_hops(n)):
            copy.wait_send()
        store(n).wait()


def solution(mesh):
    devices = mesh.shape["tp"]

    def step(x, w_gate, w_up, w_down):
        rows, model = x.shape
        hidden = w_gate.shape[1]
        tiles = model // MODEL_TILE
        dma = pltpu.SemaphoreType.DMA
        return pl.pallas_call(
            functools.partial(kernel, devices),
            out_shape=jax.ShapeDtypeStruct((rows, model), BF16),
            in_specs=[pl.BlockSpec(memory_space=pl.ANY)] * 4,
            out_specs=pl.BlockSpec(memory_space=pl.ANY),
            scratch_shapes=[
                pltpu.VMEM((model, hidden), BF16),
                pltpu.VMEM((model, hidden), BF16),
                pltpu.VMEM((hidden, model), BF16),
                pltpu.VMEM((4, 2 * rows, model), BF16),
                pltpu.VMEM((4, rows, model), BF16),
                pltpu.VMEM((rows, model), BF16),
                pltpu.VMEM((rows, model), BF16),
                pltpu.VMEM((rows, model), BF16),
                pltpu.VMEM((rows, model), BF16),
                pltpu.VMEM((rows, hidden), BF16),
                pltpu.VMEM((3, rows, hidden), BF16),
                dma((4,)),
                dma((6,)), dma((6,)), dma((4,)), dma((4,)),
                dma((4, tiles)), dma((4, tiles)),
                dma((2, tiles)), dma((2, tiles)),
                dma((2, tiles)), dma((2, tiles)),
                dma((2, tiles)), dma((2, tiles)),
                dma((tiles,)),
            ],
            compiler_params=pltpu.CompilerParams(
                collective_id=0, has_side_effects=True, vmem_limit_bytes=67_043_328
            ),
        )(x, w_gate, w_up, w_down)

    return jax.shard_map(
        step,
        mesh=mesh,
        in_specs=(P(("dp", "tp"), None), P(None, "tp"), P(None, "tp"), P("tp", None)),
        out_specs=P(("dp", "tp"), None),
        check_vma=False,
    )
```

time: 268 us -> 150 us (0.56)
  waiting for transfers between devices: 179 us -> 0 us
  Pallas kernels: 0 us -> 147 us
  matrix products: 75 us -> 0 us
  between operations: 13.4 us -> 0.01 us
  local copies, waits for them, and re-layouts: 0.01 us -> 3.09 us
    pallas_call x0 -> x1, Pallas kernels: none -> 147 us  [step(): pl.pallas_call(functools.partial(kernel, devices), out_shape=jax.ShapeDty...]
    reduce_scatter x1 -> x0, waiting for transfers between devices: 90.9 us -> none  [step(): return lax.psum_scatter(term, 'tp', scatter_dimension=0, tiled=True)]
    all_gather x1 -> x0, waiting for transfers between devices: 87.7 us -> none  [step(): rows = lax.all_gather(x, 'tp', axis=0, tiled=True)]
    dot_general x3 -> x0, matrix products: 75 us -> none  [the longest x1 26.2 us: step(): up = jnp.dot(rows, w_up, preferred_element_type=jnp.float32)]
    unnamed x2 -> x1, local copies, waits for them, and re-layouts: 0.01 us -> 3.09 us
  transfers between devices with their start and end apart: 2 -> 0, of which waited for: 2 -> 0; matrix products, arithmetic and copies ran while one was open for 0% -> 0% of each run, Pallas kernels for 0% -> 0%
where the time goes in v1:
time: 150 us
  Pallas kernels  147 us (98%)
  local copies, waits for them, and re-layouts  3.09 us (2%)
    pallas_call x1, Pallas kernels, step(): pl.pallas_call(functools.partial(kernel, devices), out_shape=jax.ShapeDty...  147 us
    unnamed x1, local copies, waits for them, and re-layouts  3.09 us

profile of v1, /device:TPU:112, one launch (start us, length us, event | category | flops | bytes accessed | tf_op | source)
XLA Modules:
  0.0 150.3 jit_solution(7811942247114966484)
XLA Ops:
  0.0 147.2 %shard_map.46 = bf16[352,3072]{1,0:T(8,128)(2,1)} custom-call(bf16[352,3072]{1,0:T(8,128)(2,1)} %x_hbm.1, bf16[3072,1024]{1,0:T(8,128)(2,1)} %wg_hbm.1, bf16[3072,1024]{1,0:T(8,128)(2,1)} %wu_hbm.1, bf16[1024,3072]{1,0:T(8,128)(2,1)} %wd_hbm.1), custom_call_target="tpu_custom_call" | custom-call | tf_op jit(solution)/shard_map/pallas_call | solution.py:219
  147.2 3.1 %copy.6 = bf16[352,3072]{1,0:T(8,128)(2,1)} copy(bf16[352,3072]{1,0:T(8,128)(2,1)} %shard_map.46) | data formatting | bytes 4325376

commit v2 on v1

v2 whole, which is shorter than its diff:
```python
import functools

import jax
import jax.numpy as jnp
from jax import lax
from jax.experimental import pallas as pl
from jax.experimental.pallas import tpu as pltpu
from jax.sharding import PartitionSpec as P

F32, BF16 = jnp.float32, jnp.bfloat16

HIDDEN_TILE = 256
MODEL_TILE = 768
LAST = 256


def tile(n, width):
    return pl.ds(pl.multiple_of(n * width, width), width)


def kernel(
    devices, x_hbm, wg_hbm, wu_hbm, wd_hbm, y,
    wg, wu, wd, xb, sib, first, pure, second, total, work, kept,
    load_sem, ag_send, ag_recv, pass_send, pass_recv,
    sib_send, sib_recv, first_send, first_recv, pure_send, pure_recv, second_send, second_recv,
):
    rows = x_hbm.shape[0]
    half = rows // 2
    hidden, model = wd.shape
    hidden_tiles, model_tiles = hidden // HIDDEN_TILE, model // MODEL_TILE
    chips = devices // 2

    me = lax.axis_index("tp")
    chip, core = me // 2, lax.rem(me, 2)
    right = {"tp": lax.rem(chip + 1, chips) * 2 + core}
    left = {"tp": lax.rem(chip + chips - 1, chips) * 2 + core}
    sibling = {"tp": chip * 2 + 1 - core}

    theirs, ours = pl.ds(0, rows), pl.ds(rows, rows)
    lo, hi = pl.ds(rows, half), pl.ds(rows + half, half)

    def remote(src, dst, send, recv, to):
        return pltpu.make_async_remote_copy(
            src_ref=src, dst_ref=dst, send_sem=send, recv_sem=recv, device_id=to, device_id_type=pl.DeviceIdType.MESH
        )

    loads = [
        pltpu.make_async_copy(src, dst, load_sem.at[i])
        for i, (src, dst) in enumerate([(x_hbm, xb.at[0, ours]), (wg_hbm, wg), (wu_hbm, wu), (wd_hbm, wd)])
    ]

    barrier = pltpu.get_barrier_semaphore()
    for peer in (left, right, sibling):
        pl.semaphore_signal(barrier, inc=1, device_id=peer, device_id_type=pl.DeviceIdType.MESH)
    pl.semaphore_wait(barrier, 3)

    top, bottom = pl.ds(0, half), pl.ds(half, half)
    early = [
        remote(x_hbm.at[top], xb.at[1, lo], ag_send.at[0], ag_recv.at[0], right),
        remote(x_hbm.at[bottom], xb.at[1, hi], ag_send.at[1], ag_recv.at[1], left),
    ]
    late = [
        remote(x_hbm.at[bottom], xb.at[2, lo], ag_send.at[2], ag_recv.at[2], right),
        remote(x_hbm.at[top], xb.at[2, hi], ag_send.at[3], ag_recv.at[3], left),
    ]
    relays = [
        remote(xb.at[1, lo], xb.at[3, lo], ag_send.at[4], ag_recv.at[4], right),
        remote(xb.at[1, hi], xb.at[3, hi], ag_send.at[5], ag_recv.at[5], left),
    ]
    passes = [
        remote(xb.at[q, ours] if q else x_hbm, xb.at[q, theirs], pass_send.at[q], pass_recv.at[q], sibling) for q in range(4)
    ]
    for copy in (*early, *late, passes[0], *loads):
        copy.start()

    def gate_up(q, keep):
        @pl.loop(0, hidden_tiles)
        def _(n):
            cols = tile(n, HIDDEN_TILE)
            gate = jnp.dot(xb[q], wg[:, cols], preferred_element_type=F32)
            up = jnp.dot(xb[q], wu[:, cols], preferred_element_type=F32)
            h = (jax.nn.silu(gate) * up).astype(BF16)
            work[:, cols] = h[:rows]
            kept[keep, :, cols] = h[rows:]

    def to_sibling(q, n):
        cols = tile(n, MODEL_TILE)
        return remote(xb.at[q, theirs, cols], sib.at[q, :, cols], sib_send.at[q, n], sib_recv.at[q, n], sibling)

    def down_theirs(q):
        @pl.loop(0, model_tiles)
        def _(n):
            cols = tile(n, MODEL_TILE)
            term = jnp.dot(work[...], wd[:, cols], preferred_element_type=F32)
            xb[q, theirs, cols] = term.astype(BF16)
            to_sibling(q, n).start()

    def from_sibling(q):
        @pl.loop(0, model_tiles)
        def _(n):
            to_sibling(q, n).wait_recv()

    def pair_sum(q, keep, cols):
        term = jnp.dot(kept[keep], wd[:, cols], preferred_element_type=F32)
        return term + sib[q, :, cols].astype(F32)

    def pure_hops():
        return (
            remote(xb.at[0, top], pure.at[top], pure_send.at[0], pure_recv.at[0], left),
            remote(xb.at[0, bottom], pure.at[bottom], pure_send.at[1], pure_recv.at[1], right),
        )

    def first_hops(n):
        cols = pl.ds(n * model // 2, model // 2)
        return (
            remote(xb.at[3, lo, cols], first.at[bottom, cols], first_send.at[0, n], first_recv.at[0, n], right),
            remote(xb.at[3, hi, cols], first.at[top, cols], first_send.at[1, n], first_recv.at[1, n], left),
        )

    ends = [(0, model // 2), (model // 2, model - LAST), (model - LAST, model)]
    pieces = [[pl.ds(c, min(MODEL_TILE, end - c)) for c in range(start, end, MODEL_TILE)] for start, end in ends]

    def second_hops(n):
        cols = pl.ds(ends[n][0], ends[n][1] - ends[n][0])
        return (
            remote(xb.at[2, lo, cols], second.at[bottom, cols], second_send.at[0, n], second_recv.at[0, n], left),
            remote(xb.at[2, hi, cols], second.at[top, cols], second_send.at[1, n], second_recv.at[1, n], right),
        )

    for load in loads:
        load.wait()
    passes[0].wait_recv()
    gate_up(0, 0)
    down_theirs(0)

    for copy in early:
        copy.wait_recv()
    for copy in (*relays, passes[1]):
        copy.start()
    passes[1].wait_recv()
    gate_up(1, 2)
    down_theirs(1)
    from_sibling(1)

    @pl.loop(0, model_tiles)
    def _(n):
        cols = tile(n, MODEL_TILE)
        to_sibling(0, n).wait_send()
        xb[0, theirs, cols] = pair_sum(1, 2, cols).astype(BF16)

    for copy in pure_hops():
        copy.start()

    for copy in late:
        copy.wait_recv()
    passes[2].start()
    passes[2].wait_recv()
    gate_up(2, 1)
    down_theirs(2)

    for copy in relays:
        copy.wait_recv()
    passes[3].start()
    passes[3].wait_recv()
    gate_up(3, 2)
    down_theirs(3)
    passes[3].wait_send()
    from_sibling(3)

    for n in range(2):

        @pl.loop(n * model_tiles // 2, (n + 1) * model_tiles // 2)
        def _(m):
            cols = tile(m, MODEL_TILE)
            xb[3, ours, cols] = pair_sum(3, 2, cols).astype(BF16)

        for copy in first_hops(n):
            copy.start()

    passes[2].wait_send()
    from_sibling(2)
    for n, columns in enumerate(pieces):
        for i, cols in enumerate(columns):
            held = pair_sum(2, 1, cols)
            if n < 2 and i == 0:
                for copy in first_hops(n):
                    copy.wait_recv()
            xb[2, ours, cols] = (held + first[:, cols].astype(F32)).astype(BF16)
        for copy in second_hops(n):
            copy.start()

    from_sibling(0)
    for copy in pure_hops():
        copy.wait_recv()

    @pl.loop(0, model_tiles)
    def _(n):
        cols = tile(n, MODEL_TILE)
        total[:, cols] = pair_sum(0, 0, cols) + pure[:, cols].astype(F32)

    for n, columns in enumerate(pieces):
        for copy in second_hops(n):
            copy.wait_recv()
        for cols in columns:
            y[:, cols] = (total[:, cols] + second[:, cols].astype(F32)).astype(BF16)

    for copy in (*early, *late, *relays, *passes[:2], *pure_hops(), *first_hops(0), *first_hops(1)):
        copy.wait_send()
    for n in range(3):
        for copy in second_hops(n):
            copy.wait_send()

    @pl.loop(0, model_tiles)
    def _(n):
        for q in range(1, 4):
            to_sibling(q, n).wait_send()


def solution(mesh):
    devices = mesh.shape["tp"]

    def step(x, w_gate, w_up, w_down):
        rows, model = x.shape
        hidden = w_gate.shape[1]
        tiles = model // MODEL_TILE
        dma = pltpu.SemaphoreType.DMA
        return pl.pallas_call(
            functools.partial(kernel, devices),
            out_shape=pltpu.VMEM((rows, model), BF16),
            in_specs=[pl.BlockSpec(memory_space=pl.ANY)] * 4,
            out_specs=pl.BlockSpec(memory_space=pltpu.VMEM),
            scratch_shapes=[
                pltpu.VMEM((model, hidden), BF16),
                pltpu.VMEM((model, hidden), BF16),
                pltpu.VMEM((hidden, model), BF16),
                pltpu.VMEM((4, 2 * rows, model), BF16),
                pltpu.VMEM((4, rows, model), BF16),
                pltpu.VMEM((rows, model), BF16),
                pltpu.VMEM((rows, model), BF16),
                pltpu.VMEM((rows, model), BF16),
                pltpu.VMEM((rows, model), F32),
                pltpu.VMEM((rows, hidden), BF16),
                pltpu.VMEM((3, rows, hidden), BF16),
                dma((4,)),
                dma((6,)), dma((6,)), dma((4,)), dma((4,)),
                dma((4, tiles)), dma((4, tiles)),
                dma((2, 2)), dma((2, 2)),
                dma((2,)), dma((2,)),
                dma((2, 3)), dma((2, 3)),
            ],
            compiler_params=pltpu.CompilerParams(
                collective_id=0, has_side_effects=True, vmem_limit_bytes=64_000_000
            ),
        )(x, w_gate, w_up, w_down)

    return jax.shard_map(
        step,
        mesh=mesh,
        in_specs=(P(("dp", "tp"), None), P(None, "tp"), P(None, "tp"), P("tp", None)),
        out_specs=P(("dp", "tp"), None),
        check_vma=False,
    )
```

time: 150 us -> 147 us (0.980)
  Pallas kernels: 147 us -> 145 us
  local copies, waits for them, and re-layouts: 3.09 us -> 1.34 us
    pallas_call x1, Pallas kernels: 147 us -> 145 us  [step(): pl.pallas_call(functools.partial(kernel, devices), out_shape=pltpu.VMEM((...]
    unnamed x1, local copies, waits for them, and re-layouts: 3.09 us -> 1.34 us
where the time goes in v2:
time: 147 us; the launch traced here: 146 us
  Pallas kernels  145 us (99%)
    pallas_call x1, Pallas kernels, step(): pl.pallas_call(functools.partial(kernel, devices), out_shape=pltpu.VMEM((...  145 us

profile of v2, /device:TPU:112, one launch (start us, length us, event | category | flops | bytes accessed | tf_op | source)
XLA Modules:
  0.0 146.5 jit_solution(13620167691383092961)
XLA Ops:
  0.0 145.1 %shard_map.46 = bf16[352,3072]{1,0:T(8,128)(2,1)S(1)} custom-call(bf16[352,3072]{1,0:T(8,128)(2,1)} %x_hbm.1, bf16[3072,1024]{1,0:T(8,128)(2,1)} %wg_hbm.1, bf16[3072,1024]{1,0:T(8,128)(2,1)} %wu_hbm.1, bf16[1024,3072]{1,0:T(8,128)(2,1)} %wd_hbm.1), custom_call_target="tpu_custom_call" | custom-call | tf_op jit(solution)/shard_map/pallas_call | solution.py:227
  145.1 1.3 copy.6

commit v3 on v2

--- a/solution.py
+++ b/solution.py
@@ -11,7 +11,8 @@
 
 HIDDEN_TILE = 256
 MODEL_TILE = 768
-LAST = 256
+LAST = 512
+HEAD = 48
 
 
 def tile(n, width):
@@ -60,17 +61,25 @@
         remote(x_hbm.at[bottom], xb.at[1, hi], ag_send.at[1], ag_recv.at[1], left),
     ]
     late = [
-        remote(x_hbm.at[bottom], xb.at[2, lo], ag_send.at[2], ag_recv.at[2], right),
-        remote(x_hbm.at[top], xb.at[2, hi], ag_send.at[3], ag_recv.at[3], left),
+        remote(x_hbm.at[pl.ds(src + start, size)], xb.at[2, pl.ds(dst + start, size)], ag_send.at[i], ag_recv.at[i], to)
+        for i, (src, dst, to, start, size) in enumerate(
+            [
+                (half, rows, right, 0, HEAD),
+                (0, rows + half, left, 0, HEAD),
+                (half, rows, right, HEAD, half - HEAD),
+                (0, rows + half, left, HEAD, half - HEAD),
+            ],
+            2,
+        )
     ]
     relays = [
-        remote(xb.at[1, lo], xb.at[3, lo], ag_send.at[4], ag_recv.at[4], right),
-        remote(xb.at[1, hi], xb.at[3, hi], ag_send.at[5], ag_recv.at[5], left),
+        remote(xb.at[1, lo], xb.at[3, lo], ag_send.at[6], ag_recv.at[6], right),
+        remote(xb.at[1, hi], xb.at[3, hi], ag_send.at[7], ag_recv.at[7], left),
     ]
     passes = [
         remote(xb.at[q, ours] if q else x_hbm, xb.at[q, theirs], pass_send.at[q], pass_recv.at[q], sibling) for q in range(4)
     ]
-    for copy in (*early, *late, passes[0], *loads):
+    for copy in (*early, *late[:2], passes[0], *loads):
         copy.start()
 
     def gate_up(q, keep):
@@ -110,18 +119,17 @@
             remote(xb.at[0, bottom], pure.at[bottom], pure_send.at[1], pure_recv.at[1], right),
         )
 
+    pieces = [pl.ds(0, model - LAST), pl.ds(model - LAST, LAST)]
+
     def first_hops(n):
-        cols = pl.ds(n * model // 2, model // 2)
+        cols = pieces[n]
         return (
             remote(xb.at[3, lo, cols], first.at[bottom, cols], first_send.at[0, n], first_recv.at[0, n], right),
             remote(xb.at[3, hi, cols], first.at[top, cols], first_send.at[1, n], first_recv.at[1, n], left),
         )
 
-    ends = [(0, model // 2), (model // 2, model - LAST), (model - LAST, model)]
-    pieces = [[pl.ds(c, min(MODEL_TILE, end - c)) for c in range(start, end, MODEL_TILE)] for start, end in ends]
-
     def second_hops(n):
-        cols = pl.ds(ends[n][0], ends[n][1] - ends[n][0])
+        cols = pieces[n]
         return (
             remote(xb.at[2, lo, cols], second.at[bottom, cols], second_send.at[0, n], second_recv.at[0, n], left),
             remote(xb.at[2, hi, cols], second.at[top, cols], second_send.at[1, n], second_recv.at[1, n], right),
@@ -135,7 +143,7 @@
 
     for copy in early:
         copy.wait_recv()
-    for copy in (*relays, passes[1]):
+    for copy in (*relays, *late[2:], passes[1]):
         copy.start()
     passes[1].wait_recv()
     gate_up(1, 2)
@@ -150,13 +158,6 @@
 
     for copy in pure_hops():
         copy.start()
-
-    for copy in late:
-        copy.wait_recv()
-    passes[2].start()
-    passes[2].wait_recv()
-    gate_up(2, 1)
-    down_theirs(2)
 
     for copy in relays:
         copy.wait_recv()
@@ -167,25 +168,33 @@
     passes[3].wait_send()
     from_sibling(3)
 
+    @pl.loop(0, model_tiles)
+    def _(n):
+        cols = tile(n, MODEL_TILE)
+        xb[3, ours, cols] = pair_sum(3, 2, cols).astype(BF16)
+
     for n in range(2):
-
-        @pl.loop(n * model_tiles // 2, (n + 1) * model_tiles // 2)
-        def _(m):
-            cols = tile(m, MODEL_TILE)
-            xb[3, ours, cols] = pair_sum(3, 2, cols).astype(BF16)
-
         for copy in first_hops(n):
             copy.start()
 
+    for copy in late:
+        copy.wait_recv()
+    passes[2].start()
+    passes[2].wait_recv()
+    gate_up(2, 1)
+    down_theirs(2)
     passes[2].wait_send()
     from_sibling(2)
-    for n, columns in enumerate(pieces):
-        for i, cols in enumerate(columns):
-            held = pair_sum(2, 1, cols)
-            if n < 2 and i == 0:
-                for copy in first_hops(n):
-                    copy.wait_recv()
-            xb[2, ours, cols] = (held + first[:, cols].astype(F32)).astype(BF16)
+
+    @pl.loop(0, model_tiles)
+    def _(n):
+        cols = tile(n, MODEL_TILE)
+        total[:, cols] = pair_sum(2, 1, cols)
+
+    for n in range(2):
+        for copy in first_hops(n):
+            copy.wait_recv()
+        xb[2, ours, pieces[n]] = (total[:, pieces[n]] + first[:, pieces[n]].astype(F32)).astype(BF16)
         for copy in second_hops(n):
             copy.start()
 
@@ -197,23 +206,15 @@
     def _(n):
         cols = tile(n, MODEL_TILE)
         total[:, cols] = pair_sum(0, 0, cols) + pure[:, cols].astype(F32)
-
-    for n, columns in enumerate(pieces):
-        for copy in second_hops(n):
-            copy.wait_recv()
-        for cols in columns:
-            y[:, cols] = (total[:, cols] + second[:, cols].astype(F32)).astype(BF16)
+        for q in range(1, 4):
+            to_sibling(q, n).wait_send()
 
     for copy in (*early, *late, *relays, *passes[:2], *pure_hops(), *first_hops(0), *first_hops(1)):
         copy.wait_send()
-    for n in range(3):
+    for n in range(2):
         for copy in second_hops(n):
-            copy.wait_send()
-
-    @pl.loop(0, model_tiles)
-    def _(n):
-        for q in range(1, 4):
-            to_sibling(q, n).wait_send()
+            copy.wait()
+        y[:, pieces[n]] = (total[:, pieces[n]] + second[:, pieces[n]].astype(F32)).astype(BF16)
 
 
 def solution(mesh):
@@ -242,11 +243,11 @@
                 pltpu.VMEM((rows, hidden), BF16),
                 pltpu.VMEM((3, rows, hidden), BF16),
                 dma((4,)),
-                dma((6,)), dma((6,)), dma((4,)), dma((4,)),
+                dma((8,)), dma((8,)), dma((4,)), dma((4,)),
                 dma((4, tiles)), dma((4, tiles)),
                 dma((2, 2)), dma((2, 2)),
                 dma((2,)), dma((2,)),
-                dma((2, 3)), dma((2, 3)),
+                dma((2, 2)), dma((2, 2)),
             ],
             compiler_params=pltpu.CompilerParams(
                 collective_id=0, has_side_effects=True, vmem_limit_bytes=64_000_000

time: 147 us -> 146 us (level)
  no operation moved by 1% of the time
where the time goes in v3:
time: 146 us
  Pallas kernels  145 us (99%)
    pallas_call x1, Pallas kernels, step(): pl.pallas_call(functools.partial(kernel, devices), out_shape=pltpu.VMEM((...  145 us

profile of v3, /device:TPU:112, one launch (start us, length us, event | category | flops | bytes accessed | tf_op | source)
XLA Modules:
  0.0 146.4 jit_solution(406969689367012452)
XLA Ops:
  0.0 145.1 %shard_map.46 = bf16[352,3072]{1,0:T(8,128)(2,1)S(1)} custom-call(bf16[352,3072]{1,0:T(8,128)(2,1)} %x_hbm.1, bf16[3072,1024]{1,0:T(8,128)(2,1)} %wg_hbm.1, bf16[3072,1024]{1,0:T(8,128)(2,1)} %wu_hbm.1, bf16[1024,3072]{1,0:T(8,128)(2,1)} %wd_hbm.1), custom_call_target="tpu_custom_call" | custom-call | tf_op jit(solution)/shard_map/pallas_call | solution.py:228
  145.1 1.3 copy.6

commit v4 on v3

--- a/solution.py
+++ b/solution.py
@@ -51,9 +51,21 @@
     ]
 
     barrier = pltpu.get_barrier_semaphore()
-    for peer in (left, right, sibling):
+
+    def greet(peer):
         pl.semaphore_signal(barrier, inc=1, device_id=peer, device_id_type=pl.DeviceIdType.MESH)
-    pl.semaphore_wait(barrier, 3)
+
+    for peer in (left, right):
+        greet(peer)
+
+    @pl.when(core == 0)
+    def _():
+        pl.semaphore_wait(barrier, 3)
+
+    @pl.when(core == 1)
+    def _():
+        pl.semaphore_wait(barrier, 2)
+
 
     top, bottom = pl.ds(0, half), pl.ds(half, half)
     early = [
@@ -79,7 +91,15 @@
     passes = [
         remote(xb.at[q, ours] if q else x_hbm, xb.at[q, theirs], pass_send.at[q], pass_recv.at[q], sibling) for q in range(4)
     ]
-    for copy in (*early, *late[:2], passes[0], *loads):
+    greet(sibling)
+    for copy in (*early, *late[:2]):
+        copy.start()
+
+    @pl.when(core == 1)
+    def _():
+        pl.semaphore_wait(barrier, 1)
+
+    for copy in (passes[0], *loads):
         copy.start()
 
     def gate_up(q, keep):

time: 146 us -> 146 us (level)
  no operation moved by 1% of the time
where the time goes in v4:
time: 146 us
  Pallas kernels  145 us (99%)
    pallas_call x1, Pallas kernels, step(): pl.pallas_call(functools.partial(kernel, devices), out_shape=pltpu.VMEM((...  145 us

profile of v4, /device:TPU:112, one launch (start us, length us, event | category | flops | bytes accessed | tf_op | source)
XLA Modules:
  0.0 146.2 jit_solution(18008311649634293433)
XLA Ops:
  0.0 144.9 %shard_map.46 = bf16[352,3072]{1,0:T(8,128)(2,1)S(1)} custom-call(bf16[352,3072]{1,0:T(8,128)(2,1)} %x_hbm.1, bf16[3072,1024]{1,0:T(8,128)(2,1)} %wg_hbm.1, bf16[3072,1024]{1,0:T(8,128)(2,1)} %wu_hbm.1, bf16[1024,3072]{1,0:T(8,128)(2,1)} %wd_hbm.1), custom_call_target="tpu_custom_call" | custom-call | tf_op jit(solution)/shard_map/pallas_call | solution.py:248
  144.9 1.3 copy.6

commit v5 on v4

--- a/solution.py
+++ b/solution.py
@@ -23,7 +23,7 @@
     devices, x_hbm, wg_hbm, wu_hbm, wd_hbm, y,
     wg, wu, wd, xb, sib, first, pure, second, total, work, kept,
     load_sem, ag_send, ag_recv, pass_send, pass_recv,
-    sib_send, sib_recv, first_send, first_recv, pure_send, pure_recv, second_send, second_recv,
+    sib_send, sib_recv, first_send, first_recv, pure_send, pure_recv, second_send, second_recv, seen, mate,
 ):
     rows = x_hbm.shape[0]
     half = rows // 2
@@ -55,17 +55,16 @@
     def greet(peer):
         pl.semaphore_signal(barrier, inc=1, device_id=peer, device_id_type=pl.DeviceIdType.MESH)
 
-    for peer in (left, right):
-        greet(peer)
-
     @pl.when(core == 0)
     def _():
-        pl.semaphore_wait(barrier, 3)
+        greet(right)
+        pl.semaphore_wait(barrier, 2)
 
     @pl.when(core == 1)
     def _():
-        pl.semaphore_wait(barrier, 2)
-
+        greet(left)
+        greet(sibling)
+        pl.semaphore_wait(barrier, 1)
 
     top, bottom = pl.ds(0, half), pl.ds(half, half)
     early = [
@@ -91,16 +90,34 @@
     passes = [
         remote(xb.at[q, ours] if q else x_hbm, xb.at[q, theirs], pass_send.at[q], pass_recv.at[q], sibling) for q in range(4)
     ]
-    greet(sibling)
-    for copy in (*early, *late[:2]):
-        copy.start()
+
+    def tell(sem, peer):
+        pl.semaphore_signal(sem, inc=1, device_id=peer, device_id_type=pl.DeviceIdType.MESH)
+
+    @pl.when(core == 0)
+    def _():
+        tell(seen, left)
+        early[1].start()
+        late[1].start()
+        tell(mate, sibling)
+        passes[0].start()
+        pl.semaphore_wait(seen, 1)
+        early[0].start()
+        late[0].start()
 
     @pl.when(core == 1)
     def _():
-        pl.semaphore_wait(barrier, 1)
-
-    for copy in (passes[0], *loads):
-        copy.start()
+        tell(seen, right)
+        early[0].start()
+        late[0].start()
+        pl.semaphore_wait(seen, 1)
+        early[1].start()
+        late[1].start()
+        pl.semaphore_wait(mate, 1)
+        passes[0].start()
+
+    for load in loads:
+        load.start()
 
     def gate_up(q, keep):
         @pl.loop(0, hidden_tiles)
@@ -268,6 +285,7 @@
                 dma((2, 2)), dma((2, 2)),
                 dma((2,)), dma((2,)),
                 dma((2, 2)), dma((2, 2)),
+                pltpu.SemaphoreType.REGULAR, pltpu.SemaphoreType.REGULAR,
             ],
             compiler_params=pltpu.CompilerParams(
                 collective_id=0, has_side_effects=True, vmem_limit_bytes=64_000_000

time: 146 us -> 146 us (level)
  no operation moved by 1% of the time
where the time goes in v5:
time: 146 us
  Pallas kernels  144 us (99%)
    pallas_call x1, Pallas kernels, step(): pl.pallas_call(functools.partial(kernel, devices), out_shape=pltpu.VMEM((...  144 us

profile of v5, /device:TPU:112, one launch (start us, length us, event | category | flops | bytes accessed | tf_op | source)
XLA Modules:
  0.0 145.8 jit_solution(7943876624162659874)
XLA Ops:
  0.0 144.5 %shard_map.46 = bf16[352,3072]{1,0:T(8,128)(2,1)S(1)} custom-call(bf16[352,3072]{1,0:T(8,128)(2,1)} %x_hbm.1, bf16[3072,1024]{1,0:T(8,128)(2,1)} %wg_hbm.1, bf16[3072,1024]{1,0:T(8,128)(2,1)} %wu_hbm.1, bf16[1024,3072]{1,0:T(8,128)(2,1)} %wd_hbm.1), custom_call_target="tpu_custom_call" | custom-call | tf_op jit(solution)/shard_map/pallas_call | solution.py:265
  144.5 1.3 copy.6

commit v6 on v5

--- a/solution.py
+++ b/solution.py
@@ -249,9 +249,13 @@
     for copy in (*early, *late, *relays, *passes[:2], *pure_hops(), *first_hops(0), *first_hops(1)):
         copy.wait_send()
     for n in range(2):
-        for copy in second_hops(n):
-            copy.wait()
-        y[:, pieces[n]] = (total[:, pieces[n]] + second[:, pieces[n]].astype(F32)).astype(BF16)
+        for copy, half_rows in zip(second_hops(n), (bottom, top)):
+            copy.wait_recv()
+            held = total[half_rows, pieces[n]] + second[half_rows, pieces[n]].astype(F32)
+            y[half_rows, pieces[n]] = held.astype(BF16)
+
+    for copy in (*second_hops(0), *second_hops(1)):
+        copy.wait_send()
 
 
 def solution(mesh):

time: 146 us -> 146 us (level)
  no operation moved by 1% of the time
where the time goes in v6:
time: 146 us
  Pallas kernels  144 us (99%)
    pallas_call x1, Pallas kernels, step(): pl.pallas_call(functools.partial(kernel, devices), out_shape=pltpu.VMEM((...  144 us

profile of v6, /device:TPU:112, one launch (start us, length us, event | category | flops | bytes accessed | tf_op | source)
XLA Modules:
  0.0 145.8 jit_solution(7645501957533718877)
XLA Ops:
  0.0 144.4 %shard_map.46 = bf16[352,3072]{1,0:T(8,128)(2,1)S(1)} custom-call(bf16[352,3072]{1,0:T(8,128)(2,1)} %x_hbm.1, bf16[3072,1024]{1,0:T(8,128)(2,1)} %wg_hbm.1, bf16[3072,1024]{1,0:T(8,128)(2,1)} %wu_hbm.1, bf16[1024,3072]{1,0:T(8,128)(2,1)} %wd_hbm.1), custom_call_target="tpu_custom_call" | custom-call | tf_op jit(solution)/shard_map/pallas_call | solution.py:269
  144.5 1.3 copy.6

commit v7 on v6

--- a/solution.py
+++ b/solution.py
@@ -229,11 +229,11 @@
         total[:, cols] = pair_sum(2, 1, cols)
 
     for n in range(2):
-        for copy in first_hops(n):
+        for copy, onward, half_rows, dst in zip(first_hops(n), second_hops(n)[::-1], (bottom, top), (hi, lo)):
             copy.wait_recv()
-        xb[2, ours, pieces[n]] = (total[:, pieces[n]] + first[:, pieces[n]].astype(F32)).astype(BF16)
-        for copy in second_hops(n):
-            copy.start()
+            held = total[half_rows, pieces[n]] + first[half_rows, pieces[n]].astype(F32)
+            xb[2, dst, pieces[n]] = held.astype(BF16)
+            onward.start()
 
     from_sibling(0)
     for copy in pure_hops():

time: 146 us -> 146 us (level)
  no operation moved by 1% of the time
where the time goes in v7:
time: 146 us
  Pallas kernels  144 us (99%)
    pallas_call x1, Pallas kernels, step(): pl.pallas_call(functools.partial(kernel, devices), out_shape=pltpu.VMEM((...  144 us

profile of v7, /device:TPU:112, one launch (start us, length us, event | category | flops | bytes accessed | tf_op | source)
XLA Modules:
  0.0 145.8 jit_solution(7533225024335967953)
XLA Ops:
  0.0 144.4 %shard_map.46 = bf16[352,3072]{1,0:T(8,128)(2,1)S(1)} custom-call(bf16[352,3072]{1,0:T(8,128)(2,1)} %x_hbm.1, bf16[3072,1024]{1,0:T(8,128)(2,1)} %wg_hbm.1, bf16[3072,1024]{1,0:T(8,128)(2,1)} %wu_hbm.1, bf16[1024,3072]{1,0:T(8,128)(2,1)} %wd_hbm.1), custom_call_target="tpu_custom_call" | custom-call | tf_op jit(solution)/shard_map/pallas_call | solution.py:269
  144.5 1.3 copy.6
